TPU v7x, 128 devices: a whole 4x4x4 slice. The times are simulated.
128 devices in a mesh: pairs: 1, cols: 2 (over core), rows: 64 (over z, y, x).
Axes of the slice: x: 4, y: 4, z: 4, core: 2. Of those that a mesh axis runs over, the one named last changes fastest.
Arguments:
- C1: float32 [512, 512], P(('pairs', 'rows'), 'cols')
- C2: float32 [8192, 8192], P(('pairs', 'rows'), 'cols')
- T0: float32 [512, 8192], P(('pairs', 'rows'), 'cols')
- p: float32 [512], P(('pairs', 'rows'))
- q: float32 [8192], P(('pairs', 'cols'))
- eps: float32 [6], P('pairs')
Outputs:
- output 1: float32 [512, 8192], P(('pairs', 'rows'), 'cols')
- output 2: float32 [1], P('pairs')
All inputs are finite; a program needn't handle non-finite values.
Results may differ from a plain program's by a relative error of at most 0.001.
Values are sent between devices in bfloat16 or wider.
A program may use at most 1 GiB of HBM per device.

v0:
```python
import heapq
import itertools
import math

import jax
import jax.numpy as jnp
from jax import lax
from jax.experimental import pallas as pl
from jax.experimental.pallas import tpu as pltpu
from jax.sharding import PartitionSpec as P

SWEEPS = 10
FLAT = pl.DeviceIdType.LOGICAL
L, S = 128, 8
JB = 64
JT = JB // S
F32, BF16 = jnp.float32, jnp.bfloat16
ORDERS = ((0, 1, 2), (1, 2, 0), (2, 0, 1))
TILE_RATE = 11.4
HOP_US = 5.0
AHEAD_US = 3.0
LOG2E = 1.4426950216293335
LOG2E_REST = 1.925963e-8
PARTNER_US = 4.0
LATE = 100


def torus_of(chips):
    return {64: (4, 4, 4), S: (4, 2, 1), 16: (4, 4, 1)}[chips]


def halves(x):
    c = 4097.0 * x
    high = c - (c - x)
    return high, x - high


def quotient(a, b):
    q = a / b
    return q + (a - q * b) / b


def split3(n):
    cuts = [0, (n + 2) // 3, (2 * n + 2) // 3, n]
    return [(cuts[k], cuts[k + 1]) for k in range(3)]


def tree_plan(dims, tiles, rate, lat_us, ahead_us, shared=0):
    rings = {1: (), 2: ((1, "f", 1),), 4: ((1, "f", 1), (3, "f", -1), (2, "a", 1), (2, "b", -1))}
    msgs = []
    for color, order in enumerate(ORDERS):
        lo, hi = split3(tiles)[color]
        for dst in itertools.product(*(range(n) for n in dims)):
            used = [k for k in range(3) if dst[order[k]]]
            if not used or lo == hi:
                continue
            d = order[used[-1]]
            mid = lo + (hi - lo + (sum(dst) + color) % 2) // 2
            for at, part, sign in rings[dims[d]]:
                a, b = {"f": (lo, hi), "a": (lo, mid), "b": (mid, hi)}[part]
                if at != dst[d] or a == b:
                    continue
                src = list(dst)
                src[d] = (src[d] - sign) % dims[d]
                m = dict(id=len(msgs), color=color, src=tuple(src), dst=dst, link=(d, sign), lo=a, hi=b)
                m["us"] = (b - a) / rate
                msgs.append(m)
    into = {}
    for m in msgs:
        into.setdefault((m["color"], m["dst"]), []).append(m)
    users = [[] for _ in msgs]
    missing = []
    for m in msgs:
        deps = [e for e in into.get((m["color"], m["src"]), []) if e["lo"] < m["hi"] and m["lo"] < e["hi"]]
        missing.append(len(deps))
        for e in deps:
            users[e["id"]].append(m)
    sems, waiting = {}, {}
    for m in msgs:
        key = (m["color"] if users[m["id"]] else None, m["dst"])
        m["sem"] = sems.setdefault(key, len(sems))
        waiting.setdefault(m["sem"], []).append(m)
    pending = {k: len(group) for k, group in waiting.items()}
    way = {}

    def way_of(m):
        if m["id"] not in way:
            way[m["id"]] = m["us"] + lat_us + max([way_of(u) for u in users[m["id"]]], default=0.0)
        return way[m["id"]]

    links = sorted({m["link"] for m in msgs})
    queue = {k: [] for k in links}
    idle = dict.fromkeys(links, True)
    ready, events, ops = {}, [], []

    def put(m, now):
        ready[m["id"]] = now
        heapq.heappush(queue[m["link"]], (-way_of(m), m["id"]))

    def start(link, now):
        if idle[link] and queue[link]:
            k = heapq.heappop(queue[link])[1]
            idle[link] = False
            ops.append((max(ready[k], now - ahead_us), 1, "send", msgs[k]))
            heapq.heappush(events, (now + msgs[k]["us"], 0, k))
            heapq.heappush(events, (now + msgs[k]["us"] + lat_us, 1, k))

    for m in msgs:
        if not missing[m["id"]]:
            put(m, 0.0)
    for link in links:
        start(link, 0.0)
    left = {}
    for m in msgs:
        left[m["dst"]] = left.get(m["dst"], 0) + 1
    now = 0.0
    while events:
        now, arrived, k = heapq.heappop(events)
        m = msgs[k]
        if not arrived:
            idle[m["link"]] = True
            start(m["link"], now)
            continue
        pending[m["sem"]] -= 1
        if not pending[m["sem"]]:
            ops.append((now, 0, "wait", waiting[m["sem"]]))
        for u in users[k]:
            missing[u["id"]] -= 1
            if not missing[u["id"]]:
                put(u, now)
                start(u["link"], now)
        left[m["dst"]] -= 1
        if not left[m["dst"]]:
            slot = m["dst"][0] + dims[0] * (m["dst"][1] + dims[1] * m["dst"][2])
            ops.append((now, 0, "slot", slot))
            if slot < shared:
                ops.append((now + PARTNER_US, 0, "partner", slot))
    ops.sort(key=lambda op: op[:2])
    totals = {k: sum(m["hi"] - m["lo"] for m in msgs if m["link"] == k) for k in links}
    return dict(waits=len(sems), ops=[op[2:] for op in ops], links=links, totals=totals, end=now)


def make_kernel(dims, n_rows, n_cols, steps, sweeps):
    X, Y, Z = dims
    CH = X * Y * Z
    NR = n_rows // CH
    G = NR // S
    NT = n_rows // L
    TB = JT * NT
    HB = CH // 2
    JN = n_cols // 2 // L
    JW = JN // 2
    NT0 = G * JW
    TT0 = NT0 + 2 * G
    KJ = CH * JB
    CK = min(1024, KJ)
    CM = min(1024, KJ)
    GS = min(4, CH // 2)
    CS = max(CH * 3 // 8 // GS * GS, GS)
    NP = CH + CS
    NE, NC = (CH - CS) // GS, 2 * CS // GS
    GC = CM // JB // GS
    assert NT == 4 and n_cols == CH * L and JN == HB
    plan0 = tree_plan(dims, TT0, TILE_RATE, HOP_US - 2, AHEAD_US - 1)
    plan = tree_plan(dims, TB, TILE_RATE, HOP_US, AHEAD_US, CS)
    links = plan["links"]
    NL = len(links)
    peers = [(d, k) for d in range(3) for k in range(1, dims[d])]
    strides = (1, X, X * Y)

    def slot_of(offset):
        return offset[0] + X * offset[1] + X * Y * offset[2]

    def kernel(
        eps_ref, p_ref, c1_ref, c2_ref, t0_ref, q_ref,
        out_ref, loss_ref,
        land, kbuf, g0, tt0, tt1, c1f, c1b, c2n, c2p, bacc, lp, lprecv, bp, qf, qrep, vbuf, cbuf,
        mb, sb, fb, ub, ap, xs, xr, mss, msr, pv, ars, arr, arps, arpr, obuf, orecv, trb, loss_rows, loss_two, c2v,
        send_sem, recv_sem, fwd_ssem, fwd_rsem, credit, x_ssem, x_rsem, ms_sem, lp_sem, c1_sem, c2_sem, q_sem, ar_ssem, ar_rsem, arp_sem, o_sem, loss_sem, in_sem,
    ):
        tts = (tt0, tt1)
        chip = lax.axis_index("rows")
        core = lax.axis_index("cols")
        other = 1 - core
        pos = (lax.rem(chip, X), lax.rem(lax.div(chip, X), Y), lax.div(chip, X * Y))

        me = core * CH + chip
        partner = other * CH + chip

        def moved(d, k):
            return me + (lax.rem(pos[d] + k + dims[d], dims[d]) - pos[d]) * strides[d]

        near = {link: moved(*link) for link in links}

        def source_of(slot):
            off = (lax.rem(slot, X), lax.rem(lax.div(slot, X), Y), lax.div(slot, X * Y))
            at = [lax.rem(pos[d] + dims[d] - off[d], dims[d]) for d in range(3)]
            return at[0] + X * at[1] + X * Y * at[2]

        def to_partner(src, dst, ssem, rsem):
            return pltpu.make_async_remote_copy(
                src_ref=src, dst_ref=dst, send_sem=ssem, recv_sem=rsem,
                device_id=partner, device_id_type=FLAT,
            )

        def tree_copy(buf, width, first, m):
            n = m["hi"] - m["lo"]
            return pltpu.make_async_remote_copy(
                src_ref=buf.at[pl.ds((first + slot_of(m["src"])) * width + m["lo"], n)],
                dst_ref=buf.at[pl.ds((first + slot_of(m["dst"])) * width + m["lo"], n)],
                send_sem=send_sem.at[links.index(m["link"])],
                recv_sem=recv_sem.at[m["sem"]],
                device_id=near[m["link"]],
                device_id_type=FLAT,
            )

        def tree(buf, width, first, the_plan, before_send=None, on_slot=None, fillers=()):
            fillers, ready, waits = list(fillers), [], 0
            for op, m in the_plan["ops"]:
                if op == "send":
                    if before_send is not None:
                        before_send(m)
                    tree_copy(buf, width, first, m).start()
                elif op == "wait":
                    while fillers and not fillers[0][0]:
                        fillers.pop(0)[1]()
                    if not ready and fillers and waits >= fillers[0][0]:
                        fillers.pop(0)[1]()
                    while ready:
                        on_slot(*ready.pop(0))
                    n = sum(e["hi"] - e["lo"] for e in m)
                    ref = buf.at[pl.ds((first + slot_of(m[0]["dst"])) * width, n)]
                    pltpu.make_async_copy(ref, ref, recv_sem.at[m[0]["sem"]]).wait()
                    waits += 1
                elif on_slot is not None:
                    ready.append((op, m))
            for at in ready:
                on_slot(*at)
            for _, f in fillers:
                f()

        def tree_sent(buf, the_plan):
            for k, link in enumerate(links):
                n = the_plan["totals"][link]
                ref = buf.at[pl.ds(0, n)]
                pltpu.make_async_copy(ref, ref, send_sem.at[k]).wait()

        def give_credit():
            for d, sign in links:
                pl.semaphore_signal(credit, inc=1, device_id=moved(d, -sign), device_id_type=FLAT)

        def all_sum_send(stage):
            for n, k in enumerate(range(1, dims[stage])):
                pltpu.make_async_remote_copy(
                    src_ref=ars.at[stage], dst_ref=arr.at[stage, n],
                    send_sem=ar_ssem.at[stage, n], recv_sem=ar_rsem.at[stage, n],
                    device_id=moved(stage, k), device_id_type=FLAT,
                ).start()

        def all_sum_get(stage):
            total = ars[stage]
            for n, k in enumerate(range(1, dims[stage])):
                pltpu.make_async_remote_copy(
                    src_ref=ars.at[stage], dst_ref=arr.at[stage, n],
                    send_sem=ar_ssem.at[stage, n], recv_sem=ar_rsem.at[stage, n],
                    device_id=moved(stage, k), device_id_type=FLAT,
                ).wait()
                total = total + arr[stage, n]
            return total

        def all_sum_step(stage):
            total = all_sum_get(stage)
            if stage < 2:
                ars[stage + 1] = total
                all_sum_send(stage + 1)
            else:
                arps[...] = total
                to_partner(arps, arpr, arp_sem.at[0], arp_sem.at[1]).start()

        c2_in = pltpu.make_async_copy(c2_ref, c2v, in_sem.at[0])
        c2_in.start()
        barrier = pltpu.get_barrier_semaphore()
        for d, k in peers:
            pl.semaphore_signal(barrier, inc=1, device_id=moved(d, k), device_id_type=FLAT)
        pl.semaphore_signal(barrier, inc=1, device_id=partner, device_id_type=FLAT)

        row = lax.broadcasted_iota(jnp.int32, (S, L), 0)
        lane = lax.broadcasted_iota(jnp.int32, (S, L), 1)

        for g in range(G):
            rows = slice(g * S, g * S + S)
            pair = jnp.concatenate([c1_ref[rows, :L], c1_ref[rows, L:]], axis=0)
            g0[NT0 + core * G + g] = pair.astype(BF16)
        c1_copy = to_partner(
            g0.at[pl.ds(NT0 + core * G, G)], g0.at[pl.ds(NT0 + core * G, G)], c1_sem.at[0], c1_sem.at[1]
        )
        q_copy = to_partner(q_ref, qf.at[pl.ds(core * HB, HB)], q_sem.at[0], q_sem.at[1])

        tile = jnp.zeros((S, L), F32)
        for t in range(2):
            part = jnp.zeros((1, L), F32)
            for k in range(NR):
                entry = c1_ref[k : k + 1, t * L : t * L + L]
                part = part + entry * entry * p_ref[k]
            tile = jnp.where(row == 2 * core + t, jnp.broadcast_to(part, (S, L)), tile)
        where = (row - 4) * L + lane
        for k in range(NR):
            tile = jnp.where(where == chip * NR + k, p_ref[k], tile)
        ars[0] = tile
        for g in range(G):
            rows = slice(g * S, g * S + S)
            for t in range(JW):
                a, b = t0_ref[rows, (2 * L) * t : (2 * L) * t + L], t0_ref[rows, (2 * L) * t + L : (2 * L) * t + (2 * L)]
                g0[g * JW + t] = jnp.concatenate([a, b], axis=0).astype(BF16)
        qf[pl.ds(core * HB, HB)] = q_ref[...]

        c2_copy = to_partner(c2n.at[pl.ds(core * HB, HB)], c2n.at[pl.ds(core * HB, HB)], c2_sem.at[0], c2_sem.at[1])
        bp[...] = jnp.zeros_like(bp)

        def round_c2(first, last):
            c2_in.wait()
            for t in range(first, last):
                blk = c2v[:, t * L : t * L + L]
                c2n[core * HB + t] = blk.astype(BF16)
                bp[...] += blk * blk * q_ref[t : t + 1, :]

        def finish_b():
            bp[...] = jnp.broadcast_to(jnp.sum(bp[...], axis=1, keepdims=True), (L, L))

        with jax.named_scope("barrier"):
            pl.semaphore_wait(barrier, len(peers) + 1)
        give_credit()
        c1_copy.start()
        q_copy.start()
        all_sum_send(0)

        src = lax.broadcasted_iota(jnp.int32, (L, L), 0)
        dst = lax.broadcasted_iota(jnp.int32, (L, L), 1)
        picks = [
            jnp.where((src - core * JB == dst - h * JB) & (dst >= h * JB) & (dst < h * JB + JB), 1.0, 0.0).astype(BF16)
            for h in range(2)
        ]

        def order_c2(first, last):
            for t in range(first, last):
                a = jnp.dot(c2n[source_of(2 * t)], picks[0], preferred_element_type=F32)
                b = jnp.dot(c2n[source_of(2 * t + 1)], picks[1], preferred_element_type=F32)
                c2p[:, t * L : t * L + L] = (a + b).astype(BF16)

        def order_q(first, last):
            def four(n, carry):
                for k in range(4):
                    p = 4 * n + k
                    shared = p < CS
                    half = jnp.where(shared, other, core)
                    line = jnp.broadcast_to(qf[pl.ds(source_of(jnp.where(shared, p, p - CS)), 1), :], (S, L))
                    for jt in range(JT):
                        own = jnp.where(lane == half * JB + jt * S + row, line, 0.0)
                        qrep[p, jt] = jnp.broadcast_to(jnp.sum(own, axis=1, keepdims=True), (S, L))
                return carry

            lax.fori_loop(first // 4, last // 4, four, 0)

        def span(n, parts, f):
            cuts = [n * k // parts for k in range(parts + 1)]
            return [lambda a=a, b=b: f(a, b) for a, b in zip(cuts, cuts[1:])]

        fillers = [(0, lambda: round_c2(0, HB)), (0, finish_b), (0, lambda: c2_copy.start())]
        fillers += [(0, lambda: q_copy.wait()), (0, lambda: order_q(0, NP)), (LATE // 2, lambda: all_sum_step(0))]
        fillers += [(LATE, lambda: all_sum_step(1))]
        waited = []

        def before_send(m):
            if not waited and m["hi"] > NT0:
                waited.append(1)
                c1_copy.wait()

        def unpack(op, s):
            chip_s = source_of(s)
            for g in range(G):
                tiles = g0[s * TT0 + g * JW : s * TT0 + g * JW + JW].astype(F32).reshape(JN, S, L)
                kbuf[pl.ds((chip_s * G + g) * JN, JN)] = tiles
                at = pl.ds(pl.multiple_of(chip_s * NR + g * S, S), S)
                for h in range(2):
                    pair = g0[s * TT0 + NT0 + h * G + g].astype(F32)
                    c1f[at, 2 * L * h : 2 * L * h + L] = pair[:S]
                    c1f[at, 2 * L * h + L : 2 * L * h + 2 * L] = pair[S:]

        with jax.named_scope("gather0"):
            first = [(0, lambda: unpack("slot", 0))]
            tree(g0, TT0, 0, plan0, before_send=before_send, on_slot=unpack, fillers=first + fillers)
            tree_sent(g0, plan0)
            c1b[...] = c1f[...].astype(BF16)
            all_sum_step(2)

        def finish_lp():
            lp[...] = jnp.concatenate([bp[...]] * NT, axis=1) - 2.0 * bacc[...]

        bacc[...] = jnp.zeros_like(bacc)
        JC = CK // L

        def first_chunk(n, carry):
            cols = []
            for t in range(JC):
                cols.append(kbuf[pl.ds(n * JC + t, CH * G, stride=JN)].reshape(n_rows, L))
            plan_c = jnp.concatenate(cols, axis=1).astype(BF16)
            lead = jnp.dot(c1b[...], plan_c, preferred_element_type=F32).astype(BF16)
            c2c = jnp.concatenate([c2n[core * HB + n * JC + t] for t in range(JC)], axis=1)
            bacc[...] += lax.dot_general(c2c, lead, (((1,), (1,)), ((), ())), preferred_element_type=F32)
            return carry

        with jax.named_scope("firstmm"):
            lax.fori_loop(0, KJ // CK, first_chunk, 0)
            finish_lp()
        to_partner(arps, arpr, arp_sem.at[0], arp_sem.at[1]).wait()
        ap[...] = jnp.where(row < 4, arps[...] + arpr[...], arps[...])
        for t in range(NT):
            pv[t] = jnp.broadcast_to(ap[4 + t : 5 + t, :], (S, L))


        def lead_and_cross(n, plan_c):
            lead = jnp.dot(plan_c[...], c1b[...], preferred_element_type=F32).astype(BF16)
            bacc[...] += jnp.dot(c2p[:, n * CM : n * CM + CM], lead, preferred_element_type=F32)

        def costs():
            copy = to_partner(lp.at[pl.ds(other * JB, JB)], lprecv, lp_sem.at[0], lp_sem.at[1])
            copy.start()
            copy.wait()
            own = lp[pl.ds(pl.multiple_of(core * JB, JB), JB), :] + lprecv[...]
            return own + jnp.concatenate([ap[t : t + 1, :] for t in range(NT)], axis=1)

        def block(s):
            return kbuf[pl.ds(s * TB, TB)].reshape(JT, NT, S, L)

        def weighted(kk, u):
            w = (kk[:, 0] * u[0] + kk[:, 1] * u[1]) + (kk[:, 2] * u[2] + kk[:, 3] * u[3])
            return jnp.sum(w, axis=2, keepdims=True)

        def passes(u, rescale=False, par=0):
            def place(g):
                return g * GS + 2 * CS if not isinstance(g, int) or g < NE else (g - NE) * GS

            def one(at, buf):
                for k in range(GS):
                    p = at + k
                    kk = block(p)
                    if rescale:
                        kk = kk * fb[:, pl.ds(p, 1), :][None]
                        kbuf[pl.ds(p * TB, TB)] = kk.reshape(TB, S, L)
                    cbuf[buf, k] = qrep[p] / jnp.broadcast_to(weighted(kk, u), (JT, S, L))

            def two(at, buf, acc):
                for k in range(GS):
                    p = at + k
                    acc = acc + jnp.sum(block(p) * cbuf[buf, k][:, None], axis=0)
                return acc

            def run(a, b, end):
                shift = place(a) - a * GS
                even, odd = a % 2, (a + 1) % 2
                pairs = max(0, (b - a - 1) // 2)

                def both(n, acc):
                    at = (a + 2 * n) * GS + shift
                    one(at + GS, odd)
                    acc = two(at, even, acc)
                    one(at + 2 * GS, even)
                    return two(at + GS, odd, acc)

                acc = lax.fori_loop(0, pairs, both, jnp.zeros((NT, S, L), F32))
                for g in range(a + 2 * pairs, b):
                    if g + 1 < end:
                        one(place(g + 1), (g + 1) % 2)
                    acc = two(place(g), g % 2, acc)
                return acc

            one(place(0), 0)
            xs[par] = run(0, NE, NE + NC)
            copy = to_partner(xs.at[par], xr.at[par], x_ssem.at[par], x_rsem.at[par])
            copy.start()
            acc = run(NE, NE + NC, NE + NC)
            copy.wait()
            total = jnp.sum((xs[par] + xr[par]) + acc, axis=1, keepdims=True)
            return quotient(pv[...], jnp.broadcast_to(total, (NT, S, L)))

        def plan_chunk(n, dst, u):
            def one(g):
                for k in range(GS):
                    p = CS + (n * GC + g) * GS + k
                    cbuf[g % 2, k] = quotient(qrep[p], jnp.broadcast_to(weighted(block(p), u), (JT, S, L)))

            one(0)
            for g in range(GC):
                if g + 1 < GC:
                    one(g + 1)
                for k in range(GS):
                    s = (n * GC + g) * GS + k
                    v = cbuf[g % 2, k]
                    vbuf[s] = v
                    t = (block(CS + s) * u[None]) * v[:, None]
                    flat = jnp.concatenate([t[:, i].reshape(JB, L) for i in range(NT)], axis=1)
                    at = (g * GS + k) * JB
                    dst[at : at + JB, :] = flat.astype(BF16)

        def outer(r, carry):
            eps = eps_ref[r]
            inv = 1.0 / eps
            inv = inv * (2.0 - eps * inv)
            main = LOG2E * inv
            (e0, e1), (m0, m1) = halves(eps), halves(main)
            prod = eps * main
            low_part = ((e0 * m0 - prod) + (e0 * m1 + e1 * m0)) + e1 * m1
            rest = (((LOG2E - prod) - low_part) + LOG2E_REST) * inv

            def decay(x):
                return jnp.exp2(x * main + x * rest)

            cost = costs()
            for jt in range(JT):
                for t in range(NT):
                    land[CS * TB + jt * NT + t] = cost[jt * S : jt * S + S, t * L : t * L + L]

            def exps(p):
                ll = land[p * TB : p * TB + TB].reshape(JT, NT, S, L)
                low = jnp.min(jnp.min(ll, axis=0), axis=1, keepdims=True)
                kk = decay(low[None] - ll)
                kbuf[p * TB : p * TB + TB] = kk.reshape(TB, S, L)
                mb[:, p : p + 1, :] = low
                sb[:, p : p + 1, :] = jnp.sum(jnp.sum(kk, axis=0), axis=1, keepdims=True)

            def passed_on(s):
                return to_partner(
                    land.at[pl.ds((CS + s) * TB, TB)], land.at[pl.ds(s * TB, TB)], fwd_ssem.at[0], fwd_rsem.at[s]
                )

            def on_slot(op, s):
                if op == "slot":
                    if s < CS:
                        passed_on(s).start()
                    exps(CS + s)
                else:
                    passed_on(s).wait_recv()
                    exps(s)

            def once(n, f):
                @pl.when(r == 0)
                def _():
                    if not n:
                        c2_copy.wait()
                    f()

            with jax.named_scope("gather"):
                pl.semaphore_wait(credit, NL)
                first = [(0, lambda: on_slot("slot", 0)), (plan["waits"] // 4, lambda: on_slot("partner", 0))]
                for n, f in enumerate(span(CH // 2, S, order_c2)):
                    first.append((LATE // 2 + 2 * n, lambda n=n, f=f: once(n, f)))
                tree(land, TB, CS, plan, on_slot=on_slot, fillers=first)
                tree_sent(land, plan)
                ref = land.at[pl.ds(0, CS * TB)]
                pltpu.make_async_copy(ref, ref, fwd_ssem.at[0]).wait()
                give_credit()

            with jax.named_scope("minx"):
                def least_of(a, b):
                    low = jnp.min(mb[:, a:b], axis=1, keepdims=True)
                    part = jnp.sum(sb[:, a:b] * decay(low - mb[:, a:b]), axis=1, keepdims=True)
                    return jnp.broadcast_to(low, (NT, S, L)), jnp.broadcast_to(part, (NT, S, L))

                mss[0], mss[1] = least_of(2 * CS, NP)
                copy = to_partner(mss, msr, ms_sem.at[0], ms_sem.at[1])
                copy.start()
                low, part = least_of(0, 2 * CS)
                copy.wait()
                least = jnp.minimum(jnp.minimum(mss[0], msr[0]), low)
                total = mss[1] * decay(least - mss[0]) + msr[1] * decay(least - msr[0])
                total = total + part * decay(least - low)
                fb[...] = decay(least[:, :1] - mb[...])
                u = quotient(pv[...], total)

            with jax.named_scope("pass1"):
                u = passes(u, rescale=True, par=1)

            def sweep(t, u):
                return passes(u, par=lax.rem(t, 2))

            with jax.named_scope("sweeps"):
                u = lax.fori_loop(2, sweeps, sweep, u)
            ub[...] = u
            bacc[...] = jnp.zeros_like(bacc)
            with jax.named_scope("finish"):
                plan_chunk(0, tts[0], u)
                for n in range(KJ // CM):
                    if n + 1 < KJ // CM:
                        plan_chunk(n + 1, tts[(n + 1) % 2], u)
                    lead_and_cross(n, tts[n % 2])
                finish_lp()
            return carry

        lax.fori_loop(0, steps, outer, 0)

        pl.semaphore_wait(credit, NL)
        u = ub[...]
        v = (vbuf[0], quotient(qrep[0], jnp.broadcast_to(weighted(block(0), u), (JT, S, L))))
        total = jnp.zeros((S, L), F32)
        for own, (p, half) in enumerate(((CS, core), (0, other))):
            plan_b = (block(p) * u[None]) * v[own][:, None]
            part = lp[pl.ds(pl.multiple_of(half * JB, JB), JB), :]
            for jt in range(JT):
                for t in range(NT):
                    cost = part[jt * S : jt * S + S, t * L : t * L + L]
                    total = total + (cost if own else cost + ap[t : t + 1, :]) * plan_b[jt, t]
        loss_rows[0:1] = jnp.sum(total, axis=0, keepdims=True)

        steps_on = [[moved(d, k) - me for k in range(dims[d])] for d in range(3)]
        offsets = sorted(itertools.product(*(range(n) for n in dims)), key=lambda o: -sum(min(k, 4 - k) for k in o))
        for o in offsets[:-1]:
            pltpu.make_async_remote_copy(
                src_ref=loss_rows.at[pl.ds(0, 1)], dst_ref=loss_rows.at[pl.ds(slot_of(o), 1)],
                send_sem=loss_sem.at[0], recv_sem=loss_sem.at[1],
                device_id=me + steps_on[0][o[0]] + steps_on[1][o[1]] + steps_on[2][o[2]], device_id_type=FLAT,
            ).start()

        it = lax.div(chip * NR, L)
        inside = pl.multiple_of(lax.rem(chip * NR, L), S)

        def rows_of(n, carry):
            for k in range(4):
                s = 4 * n + k
                kk = jnp.concatenate([kbuf[(CS + s) * TB + jt * NT + it] for jt in range(JT)], axis=0)
                uu = jnp.concatenate([ub[it]] * JT, axis=0)
                t = (kk * uu) * vbuf[s].reshape(JB, L)
                none = jnp.zeros_like(t)
                both = jnp.where(core == 0, jnp.concatenate([t, none], axis=0), jnp.concatenate([none, t], axis=0))
                trb[k] = both.T
                obuf[source_of(s)] = trb[k, pl.ds(inside, NR), :]
            return carry

        with jax.named_scope("tail"):
            lax.fori_loop(0, CH // 4, rows_of, 0)
            o_copy = to_partner(obuf.at[pl.ds(other * HB, HB)], orecv, o_sem.at[0], o_sem.at[1])
            o_copy.start()
            o_copy.wait()
            orecv[...] = obuf[pl.ds(core * HB, HB)] + orecv[...]
            o_out = pltpu.make_async_copy(orecv, out_ref, in_sem.at[1])
            o_out.start()
            ref = loss_rows.at[pl.ds(1, CH - 1)]
            pltpu.make_async_copy(ref, ref, loss_sem.at[0]).wait()
            pltpu.make_async_copy(ref, ref, loss_sem.at[1]).wait()
            loss_two[0:1] = jnp.sum(loss_rows[...], axis=0, keepdims=True)
            copy = to_partner(loss_two.at[pl.ds(0, 1)], loss_two.at[pl.ds(1, 1)], loss_sem.at[2], loss_sem.at[3])
            copy.start()
            copy.wait()
            loss_ref[0] = jnp.sum(loss_two[...])
            o_out.wait()

    vm = pltpu.VMEM
    dma = pltpu.SemaphoreType.DMA
    scratch = [
        vm((NP * TB, S, L), F32),
        vm((NP * TB, S, L), F32),
        vm((CH * TT0, 16, L), BF16),
        vm((CM, n_rows), BF16),
        vm((CM, n_rows), BF16),
        vm((n_rows, n_rows), F32),
        vm((n_rows, n_rows), BF16),
        vm((CH, L, L), BF16),
        vm((L, KJ), BF16),
        vm((L, n_rows), F32),
        vm((L, n_rows), F32),
        vm((JB, n_rows), F32),
        vm((L, L), F32),
        vm((CH, L), F32),
        vm((NP, JT, S, L), F32),
        vm((CH, JT, S, L), F32),
        vm((2, GS, JT, S, L), F32),
        vm((NT, NP, L), F32),
        vm((NT, NP, L), F32),
        vm((NT, NP, L), F32),
        vm((NT, S, L), F32),
        vm((S, L), F32),
        vm((2, NT, S, L), F32),
        vm((2, NT, S, L), F32),
        vm((2, NT, S, L), F32),
        vm((2, NT, S, L), F32),
        vm((NT, S, L), F32),
        vm((3, S, L), F32),
        vm((3, 3, S, L), F32),
        vm((S, L), F32),
        vm((S, L), F32),
        vm((CH, NR, L), F32),
        vm((HB, NR, L), F32),
        vm((4, L, L), F32),
        vm((CH, L), F32),
        vm((2, L), F32),
        vm((L, n_cols // 2), F32),
        dma((NL,)),
        dma((max(plan["waits"], plan0["waits"]),)),
        dma((1,)),
        dma((CS,)),
        pltpu.SemaphoreType.REGULAR,
        dma((2,)),
        dma((2,)),
        dma((2,)),
        dma((2,)),
        dma((2,)),
        dma((2,)),
        dma((2,)),
        dma((3, 3)),
        dma((3, 3)),
        dma((2,)),
        dma((2,)),
        dma((4,)),
        dma((2,)),
    ]
    return kernel, scratch


def solution(mesh):
    chips = mesh.shape["rows"]
    dims = torus_of(chips)
    grid_spec = P(("pairs", "rows"), "cols")

    def local_fn(c1, c2, t0, p, q, eps):
        n_rows, n_cols = p.shape[0] * chips, q.shape[0] * mesh.shape["cols"]
        kernel, scratch = make_kernel(dims, n_rows, n_cols, eps.shape[0], SWEEPS)
        vmem = pl.BlockSpec(memory_space=pltpu.VMEM)
        smem = pl.BlockSpec(memory_space=pltpu.SMEM)
        anywhere = pl.BlockSpec(memory_space=pl.ANY)
        plan, loss = pl.pallas_call(
            kernel,
            name="gromov",
            out_shape=(jax.ShapeDtypeStruct((chips // 2, t0.shape[0], L), F32), jax.ShapeDtypeStruct((1,), F32)),
            in_specs=[smem, smem, vmem, anywhere, vmem, vmem],
            out_specs=(anywhere, smem),
            scratch_shapes=scratch,
            compiler_params=pltpu.CompilerParams(
                collective_id=0, has_side_effects=True, vmem_limit_bytes=60 * 1024 * 1024
            ),
        )(eps, p, c1, c2, t0, q.reshape(chips // 2, L))
        return plan.transpose(1, 0, 2).reshape(t0.shape), loss

    return jax.shard_map(
        local_fn,
        mesh=mesh,
        in_specs=(grid_spec, grid_spec, grid_spec, P(("pairs", "rows")), P(("pairs", "cols")), P("pairs")),
        out_specs=(grid_spec, P("pairs")),
        check_vma=False,
    )
```

profile of v0, /device:TPU:1, one launch (start us, length us, event | category | flops | bytes accessed | tf_op | source)
XLA Modules:
  0.0 389.1 jit_solution(7021866499801932235)
XLA Ops:
  0.6 385.1 %gromov.1 = (f32[32,8,128]{2,1,0:T(8,128)}, f32[1]{0:T(128)}) custom-call(f32[6]{0:T(128)} %eps_ref.1, f32[8]{0:T(128)} %p_ref.1, f32[8,256]{1,0:T(8,128)} %c1_ref.1, f32[128,4096]{1,0:T(8,128)} %c2_ref.1, f32[8,4096]{1,0:T(8,128)} %t0_ref.1, f32[32,128]{1,0:T(8,128)} %bitcast.5), custom_call_target="tpu_custom_call" | custom-call | tf_op jit(solution)/shard_map/gromov/pallas_call | solution.py:729
  385.8 1.6 copy.10
where the time goes:
time: 389 us
  Pallas kernels  385 us (99%)
    pallas_call x1, Pallas kernels, local_fn(): pl.pallas_call(kernel, name='gromov', out_shape=(jax.ShapeDtypeStruct((ch...  385 us

commit v1 on v0

--- a/solution.py
+++ b/solution.py
@@ -18,7 +18,7 @@
 ORDERS = ((0, 1, 2), (1, 2, 0), (2, 0, 1))
 TILE_RATE = 11.4
 HOP_US = 5.0
-AHEAD_US = 3.0
+AHEAD_US = 2.0
 LOG2E = 1.4426950216293335
 LOG2E_REST = 1.925963e-8
 PARTNER_US = 4.0
@@ -161,7 +161,7 @@
     NE, NC = (CH - CS) // GS, 2 * CS // GS
     GC = CM // JB // GS
     assert NT == 4 and n_cols == CH * L and JN == HB
-    plan0 = tree_plan(dims, TT0, TILE_RATE, HOP_US - 2, AHEAD_US - 1)
+    plan0 = tree_plan(dims, TT0, TILE_RATE, HOP_US - 2, AHEAD_US)
     plan = tree_plan(dims, TB, TILE_RATE, HOP_US, AHEAD_US, CS)
     links = plan["links"]
     NL = len(links)
@@ -253,19 +253,18 @@
             for n, k in enumerate(range(1, dims[stage])):
                 pltpu.make_async_remote_copy(
                     src_ref=ars.at[stage], dst_ref=arr.at[stage, n],
-                    send_sem=ar_ssem.at[stage, n], recv_sem=ar_rsem.at[stage, n],
+                    send_sem=ar_ssem.at[stage], recv_sem=ar_rsem.at[stage],
                     device_id=moved(stage, k), device_id_type=FLAT,
                 ).start()
 
         def all_sum_get(stage):
-            total = ars[stage]
-            for n, k in enumerate(range(1, dims[stage])):
-                pltpu.make_async_remote_copy(
-                    src_ref=ars.at[stage], dst_ref=arr.at[stage, n],
-                    send_sem=ar_ssem.at[stage, n], recv_sem=ar_rsem.at[stage, n],
-                    device_id=moved(stage, k), device_id_type=FLAT,
-                ).wait()
-                total = total + arr[stage, n]
+            total, n = ars[stage], dims[stage] - 1
+            if n:
+                ref = arr.at[stage, pl.ds(0, n)]
+                pltpu.make_async_copy(ref, ref, ar_ssem.at[stage]).wait()
+                pltpu.make_async_copy(ref, ref, ar_rsem.at[stage]).wait()
+            for k in range(n):
+                total = total + arr[stage, k]
             return total
 
         def all_sum_step(stage):
@@ -705,8 +704,8 @@
         dma((2,)),
         dma((2,)),
         dma((2,)),
-        dma((3, 3)),
-        dma((3, 3)),
+        dma((3,)),
+        dma((3,)),
         dma((2,)),
         dma((2,)),
         dma((4,)),

time: 389 us -> 389 us (level)
  no operation moved by 1% of the time
where the time goes in v1:
time: 389 us
  Pallas kernels  385 us (99%)
    pallas_call x1, Pallas kernels, local_fn(): pl.pallas_call(kernel, name='gromov', out_shape=(jax.ShapeDtypeStruct((ch...  385 us

profile of v1, /device:TPU:1, one launch (start us, length us, event | category | flops | bytes accessed | tf_op | source)
XLA Modules:
  0.0 389.0 jit_solution(14018822278969070827)
XLA Ops:
  0.6 385.0 %gromov.1 = (f32[32,8,128]{2,1,0:T(8,128)}, f32[1]{0:T(128)}) custom-call(f32[6]{0:T(128)} %eps_ref.1, f32[8]{0:T(128)} %p_ref.1, f32[8,256]{1,0:T(8,128)} %c1_ref.1, f32[128,4096]{1,0:T(8,128)} %c2_ref.1, f32[8,4096]{1,0:T(8,128)} %t0_ref.1, f32[32,128]{1,0:T(8,128)} %bitcast.5), custom_call_target="tpu_custom_call" | custom-call | tf_op jit(solution)/shard_map/gromov/pallas_call | solution.py:728
  385.6 1.6 copy.10
